TPU v7x, 32 devices: a whole 2x2x4 slice. The times are simulated.
32 devices in a mesh: fsdp: 8 (over z, x), tp: 4 (over y, core).
Axes of the slice: x: 2, y: 2, z: 4, core: 2. Of those that a mesh axis runs over, the one named last changes fastest.
Arguments:
- slopes_in: float32 [32, 128, 4096], P(None, 'fsdp', 'tp'), may hold values from -6 to 6
- moments_in: float32 [32, 128, 4096], P(None, 'fsdp', 'tp'), may hold values from -6 to 6
- weights_in: float32 [32, 128, 4096], P(None, 'fsdp', 'tp'), may hold values from -0.1875 to 0.1875
Outputs:
- new_weights: float32 [32, 128, 4096], P(None, 'fsdp', 'tp')
- new_momentum: float32 [32, 128, 4096], P(None, 'fsdp', 'tp')
All inputs are finite; a program needn't handle non-finite values.
Results may differ from a plain program's by a relative error of at most 0.00021.
Values sent between devices are 32-bit elements; how exact they have to be, the bound alone decides.
A program may use at most 128 MiB of HBM per device.

v0:
```python
import functools

import jax
import jax.numpy as jnp
from jax import lax
from jax.experimental import pallas as pl
from jax.experimental.pallas import tpu as pltpu
from jax.sharding import PartitionSpec as P

ITERS = 5
HIGH = lax.Precision.HIGHEST
MESH = pl.DeviceIdType.MESH


hold_rate = 0.8
learn_rate = 1.0


def polynomial(gram, dot, trace):
    side = gram.shape[-1]
    eye = jnp.where(
        lax.broadcasted_iota(jnp.int32, (side, side), 0) == lax.broadcasted_iota(jnp.int32, (side, side), 1), 1.0, 0.0
    ).astype(gram.dtype)
    scale = lax.rsqrt(trace(gram * eye) + 1e-06)
    gram = gram * (scale * scale)
    total = None
    for step in range(ITERS):
        mixed = 3.4445 * eye - 4.775 * gram + 2.0315 * dot(gram, gram)
        total = mixed * scale if total is None else dot(mixed, total)
        if step < ITERS - 1:
            gram = dot(dot(mixed, gram), mixed)
    return total


def kernel(
    stages, parts, cols, slopes_ref, moments_ref, weights_ref, momentum_ref, new_ref,
    s_ref, m_ref, w_ref, back_ref, whole_ref, x_ref, y_ref, g_ref, fsend, frecv, bsend, brecv, gsend, grecv, own, out,
):
    rows = whole_ref.shape[1]
    side, wide = parts * rows, whole_ref.shape[2]
    f, t = lax.axis_index("fsdp"), lax.axis_index("tp")
    hops = sorted(range(1, parts), key=lambda k: abs(2 * k - parts))

    def load(m, which, src, dst):
        some = pl.ds(m * parts, parts)
        return pltpu.make_async_copy(src.at[some], dst.at[some], own.at[which, m])

    @pl.loop(0, stages)
    def _(m):
        load(m, 2, slopes_ref, s_ref).start()
        load(m, 3, moments_ref, m_ref).start()

    barrier = pltpu.get_barrier_semaphore()
    for k in range(1, parts):
        pl.semaphore_signal(barrier, inc=1, device_id={"fsdp": lax.rem(f + parts + k * (1 - 2 * lax.rem(t, 2)), parts)}, device_id_type=MESH)
    for k in range(1, cols):
        pl.semaphore_signal(barrier, inc=1, device_id={"tp": lax.rem(t + k, cols)}, device_id_type=MESH)
    def forward(m, peer, sender):
        return pltpu.make_async_remote_copy(
            src_ref=whole_ref.at[m * parts + peer], dst_ref=x_ref.at[m, sender],
            send_sem=fsend.at[m, peer], recv_sem=frecv.at[m, sender],
            device_id={"fsdp": peer}, device_id_type=MESH,
        )

    def backward(m, peer, sender):
        return pltpu.make_async_remote_copy(
            src_ref=y_ref.at[m, peer], dst_ref=back_ref.at[m * parts + sender],
            send_sem=bsend.at[m, peer], recv_sem=brecv.at[m, sender],
            device_id={"fsdp": peer}, device_id_type=MESH,
        )

    def partial(m, peer, sender):
        return pltpu.make_async_remote_copy(
            src_ref=g_ref.at[m, sender], dst_ref=g_ref.at[m, sender],
            send_sem=gsend.at[m, peer], recv_sem=grecv.at[m, sender],
            device_id={"tp": peer}, device_id_type=MESH,
        )

    def take(m):
        return pltpu.make_async_copy(whole_ref.at[m * parts + f], x_ref.at[m, f], own.at[5, m])

    def give(m):
        return pltpu.make_async_copy(y_ref.at[m, f], back_ref.at[m * parts + f], own.at[1, m])

    def put(m, peer):
        mat = m * parts + peer
        return pltpu.make_async_copy(w_ref.at[mat], new_ref.at[mat], out.at[m, peer])

    def finish(m, peer):
        mat = m * parts + peer
        w_ref[mat] = w_ref[mat] - learn_rate * back_ref[mat]
        put(m, peer).start()

    def add(m):
        load(m, 2, slopes_ref, s_ref).wait()
        load(m, 3, moments_ref, m_ref).wait()
        some = pl.ds(m * parts, parts)
        whole_ref[some] = hold_rate * m_ref[some] + s_ref[some]

    add(0)
    pl.semaphore_wait(barrier, parts + cols - 2)

    @pl.loop(0, stages)
    def _(m):
        @pl.when(m > 0)
        def _():
            add(m)

        for k in hops:
            forward(m, lax.rem(f + parts + k * (1 - 2 * lax.rem(t, 2)), parts), f).start()
        take(m).start()
        load(m, 4, whole_ref, momentum_ref).start()
        load(m, 0, weights_ref, w_ref).start()

    dot = functools.partial(jnp.dot, precision=HIGH, preferred_element_type=jnp.float32)

    @pl.loop(0, stages)
    def _(m):
        take(m).wait()
        for k in hops:
            peer = lax.rem(f + parts + k * (1 - 2 * lax.rem(t, 2)), parts)
            forward(m, peer, peer).wait_recv()
        x = x_ref[m].reshape(side, wide)
        g_ref[m, t] = lax.dot_general(x, x, (((1,), (1,)), ((), ())), precision=HIGH, preferred_element_type=jnp.float32)
        for k in range(1, cols):
            partial(m, lax.rem(t + k, cols), t).start()
        for k in range(1, cols):
            peer = lax.rem(t + k, cols)
            partial(m, peer, peer).wait_recv()
        gram = g_ref[m, 0]
        for k in range(1, cols):
            gram = gram + g_ref[m, k]
        total = polynomial(gram, dot, lambda a: jnp.sum(jnp.sum(a, axis=1, keepdims=True), axis=0, keepdims=True))
        y_ref[m] = dot(total, x_ref[m].reshape(side, wide)).reshape(parts, rows, wide)
        for k in hops:
            backward(m, lax.rem(f + parts + k * (1 - 2 * lax.rem(t, 2)), parts), f).start()
        give(m).start()

    @pl.loop(0, stages)
    def _(m):
        give(m).wait()
        load(m, 0, weights_ref, w_ref).wait()
        finish(m, f)
        for k in hops:
            peer = lax.rem(f + parts + k * (1 - 2 * lax.rem(t, 2)), parts)
            backward(m, peer, peer).wait_recv()
            finish(m, peer)

    @pl.loop(0, stages)
    def _(m):
        load(m, 4, whole_ref, momentum_ref).wait()
        put(m, f).wait()
        for k in hops:
            peer = lax.rem(f + parts + k * (1 - 2 * lax.rem(t, 2)), parts)
            put(m, peer).wait()
            forward(m, peer, f).wait_send()
            backward(m, peer, f).wait_send()
        for k in range(1, cols):
            partial(m, lax.rem(t + k, cols), t).wait_send()


def leave(first_ref, second_ref, first_out, second_out, sems):
    copies = [pltpu.make_async_copy(first_ref, first_out, sems.at[0]), pltpu.make_async_copy(second_ref, second_out, sems.at[1])]
    for copy in copies:
        copy.start()
    for copy in copies:
        copy.wait()


def leave_kernel(first, second):
    return pl.pallas_call(
        leave,
        out_shape=[jax.ShapeDtypeStruct(a.shape, a.dtype) for a in (first, second)],
        in_specs=[pl.BlockSpec(memory_space=pl.ANY)] * 2,
        out_specs=[pl.BlockSpec(memory_space=pl.ANY)] * 2,
        scratch_shapes=[pltpu.SemaphoreType.DMA((2,))],
        compiler_params=pltpu.CompilerParams(vmem_limit_bytes=2**20),
    )(first, second)


def iterate_kernel(slopes_in, moments_in, weights_in, parts, cols):
    mats, rows, wide = slopes_in.shape
    stages, side = mats // parts, rows * parts
    dma = pltpu.SemaphoreType.DMA
    return pl.pallas_call(
        functools.partial(kernel, stages, parts, cols),
        out_shape=[jax.ShapeDtypeStruct(slopes_in.shape, slopes_in.dtype)] * 2,
        in_specs=[pl.BlockSpec(memory_space=pltpu.HBM)] * 3,
        out_specs=[pl.BlockSpec(memory_space=pl.ANY)] * 2,
        scratch_shapes=[
            *[pltpu.VMEM((mats, rows, wide), jnp.float32)] * 5,
            pltpu.VMEM((stages, parts, rows, wide), jnp.float32),
            pltpu.VMEM((stages, parts, rows, wide), jnp.float32),
            pltpu.VMEM((stages, cols, side, side), jnp.float32),
            dma((stages, parts)), dma((stages, parts)), dma((stages, parts)), dma((stages, parts)),
            dma((stages, cols)), dma((stages, cols)), dma((6, stages)), dma((stages, parts)),
        ],
        compiler_params=pltpu.CompilerParams(collective_id=0, has_side_effects=True, vmem_limit_bytes=48 * 2**20),
    )(slopes_in, moments_in, weights_in)


def iterate_plain(new_momentum):
    moved = lax.all_to_all(new_momentum, "fsdp", split_axis=0, concat_axis=1, tiled=True)
    gram = lax.psum(jnp.einsum("mik,mjk->mij", moved, moved, precision=HIGH), "tp")
    dot = functools.partial(jnp.einsum, "mij,mjk->mik", precision=HIGH)
    total = polynomial(gram, dot, lambda a: jnp.sum(a, axis=(1, 2), keepdims=True))
    return lax.all_to_all(dot(total, moved), "fsdp", split_axis=1, concat_axis=0, tiled=True)


def body(parts, cols, slopes_in, moments_in, weights_in):
    if slopes_in.shape[1] % 8 == 0:
        new_momentum, new_weights = iterate_kernel(slopes_in, moments_in, weights_in, parts, cols)
        new_weights, new_momentum = leave_kernel(new_weights, new_momentum)
    else:
        new_momentum = hold_rate * moments_in + slopes_in
        new_weights = weights_in - learn_rate * iterate_plain(new_momentum)
    return (new_weights, new_momentum)


def solution(mesh):
    return jax.shard_map(
        functools.partial(body, mesh.shape["fsdp"], mesh.shape["tp"]),
        mesh=mesh,
        in_specs=(P(None, "fsdp", "tp"), P(None, "fsdp", "tp"), P(None, "fsdp", "tp")),
        out_specs=(P(None, "fsdp", "tp"), P(None, "fsdp", "tp")),
        check_vma=False,
    )
```

profile of v0, /device:TPU:8, one launch (start us, length us, event | category | flops | bytes accessed | tf_op | source)
XLA Modules:
  0.0 99.7 jit_solution(4507042717028845678)
XLA Ops:
  0.6 97.1 %shard_map.50 = (f32[32,16,1024]{2,1,0:T(8,128)S(1)}, f32[32,16,1024]{2,1,0:T(8,128)S(1)}) custom-call(f32[32,16,1024]{2,1,0:T(8,128)} %slopes_ref.1, f32[32,16,1024]{2,1,0:T(8,128)} %moments_ref.1, f32[32,16,1024]{2,1,0:T(8,128)} %weights_ref.1), custom_call_target="tpu_custom_call" | custom-call | tf_op jit(solution)/shard_map/pallas_call | solution.py:185
  97.7 2.0 %shard_map.51 = (f32[32,16,1024]{2,1,0:T(8,128)}, f32[32,16,1024]{2,1,0:T(8,128)}) custom-call(f32[32,16,1024]{2,1,0:T(8,128)S(1)} %get-tuple-element.4.first_ref, f32[32,16,1024]{2,1,0:T(8,128)S(1)} %get-tuple-element.5.second_ref), custom_call_target="tpu_custom_call" | custom-call | tf_op jit(solution)/shard_map/pallas_call | solution.py:171
where the time goes:
time: 101 us; the launch traced here: 99.7 us
  Pallas kernels  99.1 us (98%)
    pallas_call x1, Pallas kernels, iterate_kernel(): pl.pallas_call(functools.partial(kernel, stages, parts, cols), out_shape=...  97.1 us
    pallas_call x1, Pallas kernels, leave_kernel(): pl.pallas_call(leave, out_shape=[jax.ShapeDtypeStruct(a.shape, a.dtype) f...  2.03 us

commit v1 on v0

v1 whole, which is shorter than its diff:
```python
import functools

import jax
import jax.numpy as jnp
from jax import lax
from jax.experimental import pallas as pl
from jax.experimental.pallas import tpu as pltpu
from jax.sharding import PartitionSpec as P

ITERS = 5
HIGH = lax.Precision.HIGHEST
MESH = pl.DeviceIdType.MESH


hold_rate = 0.8
learn_rate = 1.0


def polynomial(gram, dot, trace):
    side = gram.shape[-1]
    eye = jnp.where(
        lax.broadcasted_iota(jnp.int32, (side, side), 0) == lax.broadcasted_iota(jnp.int32, (side, side), 1), 1.0, 0.0
    ).astype(gram.dtype)
    scale = lax.rsqrt(trace(gram * eye) + 1e-06)
    gram = gram * (scale * scale)
    total = None
    for step in range(ITERS):
        mixed = 3.4445 * eye - 4.775 * gram + 2.0315 * dot(gram, gram)
        total = mixed * scale if total is None else dot(mixed, total)
        if step < ITERS - 1:
            gram = dot(dot(mixed, gram), mixed)
    return total


def kernel(
    stages, parts, cols, slopes_ref, moments_ref, weights_ref, momentum_ref, new_ref,
    sm_ref, w_ref, back_ref, x_ref, y_ref, g_ref, loads, wload, fsend, frecv, bsend, brecv, blast, gsend, grecv, rounds,
):
    rows, wide = momentum_ref.shape[1:]
    side, mats, half = parts * rows, stages * parts, parts // 2
    last = stages - 1
    f, t = lax.axis_index("fsdp"), lax.axis_index("tp")
    upper = f // half

    def pair(k):
        peer = f
        for bit in range(k.bit_length()):
            if k >> bit & 1:
                peer = peer + (1 - 2 * ((f // 2**bit) % 2)) * 2**bit
        return peer

    def across(i):
        return upper * i + (1 - upper) * (parts - 1 - i)

    near = [k for k in (parts - 2, 2, 1) if 0 < k < parts]
    far = [k for k in range(parts - 1, 0, -1) if k not in near]

    def load(m, which, src):
        some = pl.ds(m * parts, parts)
        return pltpu.make_async_copy(src.at[some], sm_ref.at[which, some], loads.at[m])

    @pl.loop(0, stages)
    def _(m):
        load(m, 0, slopes_ref).start()
        load(m, 1, moments_ref).start()

    barrier = pltpu.get_barrier_semaphore()
    for k in near:
        pl.semaphore_signal(barrier, inc=1, device_id={"fsdp": pair(k)}, device_id_type=MESH)
    for k in range(1, cols):
        pl.semaphore_signal(barrier, inc=1, device_id={"tp": lax.rem(t + k, cols)}, device_id_type=MESH)

    def forward(m, peer):
        return pltpu.make_async_remote_copy(
            src_ref=momentum_ref.at[m * parts + peer], dst_ref=x_ref.at[m, f],
            send_sem=fsend.at[0], recv_sem=frecv.at[m],
            device_id={"fsdp": peer}, device_id_type=MESH,
        )

    def backward(m, peer, recv):
        return pltpu.make_async_remote_copy(
            src_ref=y_ref.at[m, peer], dst_ref=back_ref.at[m * parts + f],
            send_sem=bsend.at[0], recv_sem=recv,
            device_id={"fsdp": peer}, device_id_type=MESH,
        )

    def partial(m, peer):
        return pltpu.make_async_remote_copy(
            src_ref=g_ref.at[m * cols + t], dst_ref=g_ref.at[m * cols + t],
            send_sem=gsend.at[0], recv_sem=grecv.at[m],
            device_id={"tp": peer}, device_id_type=MESH,
        )

    def settle(ref, sem):
        pltpu.make_async_copy(ref, ref, sem).wait()

    def add(m):
        some = pl.ds(m * parts, parts)
        settle(sm_ref.at[:, some], loads.at[m])
        momentum_ref[some] = hold_rate * sm_ref[1, some] + sm_ref[0, some]
        x_ref[m, f] = hold_rate * sm_ref[1, m * parts + f] + sm_ref[0, m * parts + f]

    def greet(r):
        for k in near:
            pl.semaphore_signal(rounds.at[r], inc=1, device_id={"fsdp": pair(k)}, device_id_type=MESH)

    add(0)
    pl.semaphore_wait(barrier, len(near) + cols - 1)
    forward(0, pair(near[0])).start()
    greet(0)
    for k in near[1:]:
        forward(0, pair(k)).start()

    @pl.loop(1, stages)
    def _(m):
        add(m)
        forward(m, pair(near[0])).start()

    pl.semaphore_wait(rounds.at[0], len(near))
    greet(1)
    for k in far:
        if k != parts - 3:
            forward(0, pair(k)).start()
    pl.semaphore_wait(rounds.at[1], len(near))
    forward(0, pair(parts - 3)).start()

    @pl.loop(1, stages)
    def _(m):
        for k in range(parts - 1, 0, -1):
            if k != near[0]:
                forward(m, pair(k)).start()

    weights = pltpu.make_async_copy(weights_ref, w_ref, wload.at[0])
    weights.start()

    dot = functools.partial(jnp.dot, precision=HIGH, preferred_element_type=jnp.float32)

    @pl.loop(0, stages)
    def _(m):
        settle(x_ref.at[m, pl.ds(0, parts - 1)], frecv.at[m])
        x = x_ref[m].reshape(side, wide)
        g_ref[m * cols + t] = lax.dot_general(x, x, (((1,), (1,)), ((), ())), precision=HIGH, preferred_element_type=jnp.float32)
        for k in range(1, cols):
            partial(m, lax.rem(t + k, cols)).start()
        settle(g_ref.at[pl.ds(m * cols, cols - 1)], grecv.at[m])
        gram = g_ref[m * cols]
        for k in range(1, cols):
            gram = gram + g_ref[m * cols + k]
        total = polynomial(gram, dot, lambda a: jnp.sum(jnp.sum(a, axis=1, keepdims=True), axis=0, keepdims=True))
        y_ref[m] = dot(total, x_ref[m].reshape(side, wide)).reshape(parts, rows, wide)

        @pl.when(m < last)
        def _():
            for i in range(half):
                backward(m, across(i), brecv.at[m]).start()
            for k in range(half - 1, 0, -1):
                backward(m, pair(k), brecv.at[m]).start()

        @pl.when(m == last)
        def _():
            for k in range(half - 1, 0, -1):
                backward(m, pair(k), blast.at[f]).start()
            for i in range(half):
                backward(m, across(i), blast.at[f]).start()

    weights.wait()

    def finish(m, peer):
        mat = m * parts + peer
        new_ref[mat] = w_ref[mat] - learn_rate * back_ref[mat]

    def own(m):
        mat = m * parts + f
        new_ref[mat] = w_ref[mat] - learn_rate * y_ref[m, f]

    @pl.loop(0, last)
    def _(m):
        settle(back_ref.at[pl.ds(0, parts - 1)], brecv.at[m])
        own(m)
        for k in range(1, parts):
            finish(m, pair(k))

    own(last)
    for peer in [*[pair(k) for k in range(half - 1, 0, -1)], *[across(i) for i in range(half)]]:
        settle(back_ref.at[last * parts + peer], blast.at[peer])
        finish(last, peer)

    settle(momentum_ref.at[pl.ds(0, mats - stages)], fsend.at[0])
    settle(back_ref.at[pl.ds(0, mats - stages)], bsend.at[0])
    settle(g_ref.at[pl.ds(0, stages * (cols - 1))], gsend.at[0])


def leave(first_ref, second_ref, first_out, second_out, sems):
    copies = [pltpu.make_async_copy(first_ref, first_out, sems.at[0]), pltpu.make_async_copy(second_ref, second_out, sems.at[1])]
    for copy in copies:
        copy.start()
    for copy in copies:
        copy.wait()


def leave_kernel(first, second):
    return pl.pallas_call(
        leave,
        out_shape=[jax.ShapeDtypeStruct(a.shape, a.dtype) for a in (first, second)],
        in_specs=[pl.BlockSpec(memory_space=pl.ANY)] * 2,
        out_specs=[pl.BlockSpec(memory_space=pl.ANY)] * 2,
        scratch_shapes=[pltpu.SemaphoreType.DMA((2,))],
        compiler_params=pltpu.CompilerParams(vmem_limit_bytes=2**20),
    )(first, second)


def iterate_kernel(slopes_in, moments_in, weights_in, parts, cols):
    mats, rows, wide = slopes_in.shape
    stages, side = mats // parts, rows * parts
    dma = pltpu.SemaphoreType.DMA
    return pl.pallas_call(
        functools.partial(kernel, stages, parts, cols),
        out_shape=[jax.ShapeDtypeStruct(slopes_in.shape, slopes_in.dtype)] * 2,
        in_specs=[pl.BlockSpec(memory_space=pltpu.HBM)] * 3,
        out_specs=[pl.BlockSpec(memory_space=pltpu.VMEM)] * 2,
        scratch_shapes=[
            pltpu.VMEM((2, mats, rows, wide), jnp.float32),
            *[pltpu.VMEM((mats, rows, wide), jnp.float32)] * 2,
            *[pltpu.VMEM((stages, parts, rows, wide), jnp.float32)] * 2,
            pltpu.VMEM((stages * cols, side, side), jnp.float32),
            dma((stages,)), dma((1,)), dma((1,)), dma((stages,)), dma((1,)), dma((stages,)), dma((parts,)),
            dma((1,)), dma((stages,)), pltpu.SemaphoreType.REGULAR((2,)),
        ],
        compiler_params=pltpu.CompilerParams(collective_id=0, has_side_effects=True, vmem_limit_bytes=48 * 2**20),
    )(slopes_in, moments_in, weights_in)


def iterate_plain(new_momentum):
    moved = lax.all_to_all(new_momentum, "fsdp", split_axis=0, concat_axis=1, tiled=True)
    gram = lax.psum(jnp.einsum("mik,mjk->mij", moved, moved, precision=HIGH), "tp")
    dot = functools.partial(jnp.einsum, "mij,mjk->mik", precision=HIGH)
    total = polynomial(gram, dot, lambda a: jnp.sum(a, axis=(1, 2), keepdims=True))
    return lax.all_to_all(dot(total, moved), "fsdp", split_axis=1, concat_axis=0, tiled=True)


def body(parts, cols, slopes_in, moments_in, weights_in):
    if slopes_in.shape[1] % 8 == 0:
        new_momentum, new_weights = iterate_kernel(slopes_in, moments_in, weights_in, parts, cols)
        new_weights, new_momentum = leave_kernel(new_weights, new_momentum)
    else:
        new_momentum = hold_rate * moments_in + slopes_in
        new_weights = weights_in - learn_rate * iterate_plain(new_momentum)
    return (new_weights, new_momentum)


def solution(mesh):
    return jax.shard_map(
        functools.partial(body, mesh.shape["fsdp"], mesh.shape["tp"]),
        mesh=mesh,
        in_specs=(P(None, "fsdp", "tp"), P(None, "fsdp", "tp"), P(None, "fsdp", "tp")),
        out_specs=(P(None, "fsdp", "tp"), P(None, "fsdp", "tp")),
        check_vma=False,
    )
```

time: 101 us -> 97.4 us (0.964); the launches traced: 99.7 us -> 97.2 us
  Pallas kernels: 99.1 us -> 96.6 us
    pallas_call x1, Pallas kernels: 97.1 us -> 94.6 us  [iterate_kernel(): pl.pallas_call(functools.partial(kernel, stages, parts, cols), out_shape=...]
where the time goes in v1:
time: 97.4 us; the launch traced here: 97.2 us
  Pallas kernels  96.6 us (99%)
    pallas_call x1, Pallas kernels, iterate_kernel(): pl.pallas_call(functools.partial(kernel, stages, parts, cols), out_shape=...  94.6 us
    pallas_call x1, Pallas kernels, leave_kernel(): pl.pallas_call(leave, out_shape=[jax.ShapeDtypeStruct(a.shape, a.dtype) f...  2.03 us

profile of v1, /device:TPU:8, one launch (start us, length us, event | category | flops | bytes accessed | tf_op | source)
XLA Modules:
  0.0 97.2 jit_solution(13003285558733601219)
XLA Ops:
  0.6 94.6 %shard_map.50 = (f32[32,16,1024]{2,1,0:T(8,128)S(1)}, f32[32,16,1024]{2,1,0:T(8,128)S(1)}) custom-call(f32[32,16,1024]{2,1,0:T(8,128)} %slopes_ref.1, f32[32,16,1024]{2,1,0:T(8,128)} %moments_ref.1, f32[32,16,1024]{2,1,0:T(8,128)} %weights_ref.1), custom_call_target="tpu_custom_call" | custom-call | tf_op jit(solution)/shard_map/pallas_call | solution.py:216
  95.2 2.0 %shard_map.51 = (f32[32,16,1024]{2,1,0:T(8,128)}, f32[32,16,1024]{2,1,0:T(8,128)}) custom-call(f32[32,16,1024]{2,1,0:T(8,128)S(1)} %get-tuple-element.4.first_ref, f32[32,16,1024]{2,1,0:T(8,128)S(1)} %get-tuple-element.5.second_ref), custom_call_target="tpu_custom_call" | custom-call | tf_op jit(solution)/shard_map/pallas_call | solution.py:202

commit v2 on v1

v2 whole, which is shorter than its diff:
```python
import functools

import jax
import jax.numpy as jnp
from jax import lax
from jax.experimental import pallas as pl
from jax.experimental.pallas import tpu as pltpu
from jax.sharding import PartitionSpec as P

ITERS = 5
HIGH = lax.Precision.HIGHEST
MESH = pl.DeviceIdType.MESH


hold_rate = 0.8
learn_rate = 1.0


def polynomial(gram, dot, trace):
    side = gram.shape[-1]
    eye = jnp.where(
        lax.broadcasted_iota(jnp.int32, (side, side), 0) == lax.broadcasted_iota(jnp.int32, (side, side), 1), 1.0, 0.0
    ).astype(gram.dtype)
    scale = lax.rsqrt(trace(gram * eye) + 1e-06)
    gram = gram * (scale * scale)
    total = None
    for step in range(ITERS):
        mixed = 3.4445 * eye - 4.775 * gram + 2.0315 * dot(gram, gram)
        total = mixed * scale if total is None else dot(mixed, total)
        if step < ITERS - 1:
            gram = dot(dot(mixed, gram), mixed)
    return total


def kernel(
    stages, parts, cols, slopes_ref, moments_ref, weights_ref, momentum_ref, new_ref,
    first_ref, sm_ref, w_ref, back_ref, x_ref, y_ref, g_ref, loads, fsend, frecv, bsend, brecv, blast, gsend, grecv, met, rounds,
):
    rows, wide = momentum_ref.shape[1:]
    side, mats, half, last = parts * rows, stages * parts, parts // 2, stages - 1
    f, t = lax.axis_index("fsdp"), lax.axis_index("tp")
    upper = f // half

    def pair(k):
        peer = f
        for bit in range(k.bit_length()):
            if k >> bit & 1:
                peer = peer + (1 - 2 * ((f // 2**bit) % 2)) * 2**bit
        return peer

    near, level = neighbours(parts)
    n_rounds = max(level.values()) - 1
    if half > 2:
        outer = jnp.where((f // 2 == half // 2 - 1) | (f // 2 == half // 2), 0, 1)
    else:
        outer = f * 0 + 1
    first = near[0]
    rest = [k for k in range(parts - 1, 0, -1) if k != first]
    inside = [pair(k) for k in range(half - 1, 0, -1)]
    outside = []
    for j in range(half // 2):
        z = upper * j + (1 - upper) * (half - 1 - j)
        x = f % 2 if j == half // 2 - 1 else 1
        outside += [2 * z + 1 - x, 2 * z + x]

    def near_signal(sem):
        for k in near:
            pl.semaphore_signal(sem, inc=1, device_id={"fsdp": pair(k)}, device_id_type=MESH)

    def tp_signal(sem):
        @pl.when(outer == 1)
        def _():
            for k in range(1, cols):
                pl.semaphore_signal(sem, inc=1, device_id={"tp": lax.rem(t + k, cols)}, device_id_type=MESH)

    barrier = pltpu.get_barrier_semaphore()

    def load_first(m, sem):
        mat = m * parts + pair(first)
        pltpu.make_async_copy(slopes_ref.at[mat], first_ref.at[0, m], sem).start()
        pltpu.make_async_copy(moments_ref.at[mat], first_ref.at[1, m], sem).start()

    load_first(0, loads.at[0])
    near_signal(barrier)
    for m in range(1, stages):
        load_first(m, loads.at[1])

    tp_signal(barrier)

    def forward(m, peer):
        return pltpu.make_async_remote_copy(
            src_ref=momentum_ref.at[m * parts + peer], dst_ref=x_ref.at[m, f],
            send_sem=fsend.at[0], recv_sem=frecv.at[m],
            device_id={"fsdp": peer}, device_id_type=MESH,
        )

    def backward(m, peer, recv):
        return pltpu.make_async_remote_copy(
            src_ref=y_ref.at[m, peer], dst_ref=back_ref.at[m * parts + f],
            send_sem=bsend.at[0], recv_sem=recv,
            device_id={"fsdp": peer}, device_id_type=MESH,
        )

    def partial(m, peer):
        return pltpu.make_async_remote_copy(
            src_ref=g_ref.at[m * cols + t], dst_ref=g_ref.at[m * cols + t],
            send_sem=gsend.at[0], recv_sem=grecv.at[lax.rem(m, 2)],
            device_id={"tp": peer}, device_id_type=MESH,
        )

    def settle(ref, sem):
        pltpu.make_async_copy(ref, ref, sem).wait()

    def add(m):
        for k in [0, *rest]:
            mat = m * parts + pair(k)
            value = hold_rate * sm_ref[1, mat] + sm_ref[0, mat]
            momentum_ref[mat] = value
            if k == 0:
                x_ref[m, f] = value

    settle(first_ref.at[:, 0], loads.at[0])
    momentum_ref[pair(first)] = hold_rate * first_ref[1, 0] + first_ref[0, 0]
    for which, src in enumerate((slopes_ref, moments_ref)):
        pltpu.make_async_copy(src, sm_ref.at[which], loads.at[0]).start()
    pl.semaphore_wait(barrier, len(near) + outer * (cols - 1))
    forward(0, pair(first)).start()
    settle(first_ref.at[:, pl.ds(1, stages - 1)], loads.at[1])
    for m in range(1, stages):
        momentum_ref[m * parts + pair(first)] = hold_rate * first_ref[1, m] + first_ref[0, m]
        forward(m, pair(first)).start()
    tp_signal(met.at[0])
    if n_rounds:
        near_signal(rounds.at[0])
    settle(sm_ref, loads.at[0])
    add(0)
    for k in rest:
        if level[k] == 1:
            forward(0, pair(k)).start()

    @pl.loop(1, stages)
    def _(m):
        add(m)

    weights = pltpu.make_async_copy(weights_ref, w_ref, loads.at[1])
    weights.start()
    for r in range(n_rounds):
        pl.semaphore_wait(rounds.at[r], len(near))
        if r == n_rounds - 1:
            break
        if r == n_rounds - 2:
            @pl.when(outer == 1)
            def _():
                pl.semaphore_wait(met.at[0], cols - 1)
        near_signal(rounds.at[r + 1])
        for k in rest:
            if level[k] == r + 2:
                forward(0, pair(k)).start()
    for k in rest:
        if level[k] == n_rounds + 1 and n_rounds:
            forward(0, pair(k)).start()

    @pl.loop(1, stages)
    def _(m):
        for k in rest:
            forward(m, pair(k)).start()

    dot = functools.partial(jnp.dot, precision=HIGH, preferred_element_type=jnp.float32)

    @pl.loop(0, stages)
    def _(m):
        settle(x_ref.at[m, pl.ds(0, parts - 1)], frecv.at[m])
        x = x_ref[m].reshape(side, wide)
        g_ref[m * cols + t] = lax.dot_general(x, x, (((1,), (1,)), ((), ())), precision=HIGH, preferred_element_type=jnp.float32)
        for k in range(1, cols):
            partial(m, lax.rem(t + k, cols)).start()
        settle(g_ref.at[pl.ds(m * cols, cols - 1)], grecv.at[lax.rem(m, 2)])
        gram = g_ref[m * cols]
        for k in range(1, cols):
            gram = gram + g_ref[m * cols + k]
        total = polynomial(gram, dot, lambda a: jnp.sum(jnp.sum(a, axis=1, keepdims=True), axis=0, keepdims=True))
        y_ref[m] = dot(total, x_ref[m].reshape(side, wide)).reshape(parts, rows, wide)

        @pl.when(m < last)
        def _():
            for peer in outside[:-1] + inside:
                backward(m, peer, brecv.at[0]).start()

        @pl.when(m < last - 1)
        def _():
            backward(m, outside[-1], brecv.at[0]).start()

        @pl.when(m == last)
        def _():
            for peer in inside:
                backward(m, peer, blast.at[0]).start()
            backward(m, outside[0], blast.at[1 + f % half]).start()
            if last:
                backward(last - 1, outside[-1], brecv.at[0]).start()
            for peer in outside[1:-1]:
                backward(m, peer, blast.at[1 + f % half]).start()

            @pl.when(t % 2 == 0)
            def _():
                backward(m, outside[-1], blast.at[1 + f % half]).start()

    def finish(m, peers):
        for peer in peers:
            mat = m * parts + peer
            new_ref[mat] = w_ref[mat] - learn_rate * back_ref[mat]

    weights.wait()
    for m in range(stages):
        new_ref[m * parts + f] = w_ref[m * parts + f] - learn_rate * y_ref[m, f]
    if last:
        settle(back_ref.at[pl.ds(0, last * (parts - 1))], brecv.at[0])

        @pl.loop(0, last)
        def _(m):
            finish(m, inside + outside)

    @pl.when(t % 2 == 1)
    def _():
        settle(back_ref.at[pl.ds(0, mats - stages - 1)], bsend.at[0])
        backward(last, outside[-1], blast.at[1 + f % half]).start()

    if inside:
        settle(back_ref.at[pl.ds(0, len(inside))], blast.at[0])
        finish(last, inside)
    for peer in outside:
        settle(back_ref.at[last * parts + peer], blast.at[1 + peer % half])
        finish(last, [peer])

    settle(momentum_ref.at[pl.ds(0, mats - stages)], fsend.at[0])
    @pl.when(t % 2 == 1)
    def _():
        settle(back_ref.at[pl.ds(0, 1)], bsend.at[0])

    @pl.when(t % 2 == 0)
    def _():
        settle(back_ref.at[pl.ds(0, mats - stages)], bsend.at[0])

    settle(g_ref.at[pl.ds(0, stages * (cols - 1))], gsend.at[0])


def neighbours(parts):
    near = [k for k in (parts - 2, *(2**b for b in range(1, parts.bit_length() - 2)), 1) if k]
    near = list(dict.fromkeys(near))
    level, edge = {0: 0}, [0]
    while edge:
        found = {}
        for k in edge:
            for step in near:
                if k ^ step not in level:
                    found[k ^ step] = level[k] + 1
        level.update(found)
        edge = list(found)
    return near, level


def leave(first_ref, second_ref, first_out, second_out, sems):
    copies = [pltpu.make_async_copy(first_ref, first_out, sems.at[0]), pltpu.make_async_copy(second_ref, second_out, sems.at[1])]
    for copy in copies:
        copy.start()
    for copy in copies:
        copy.wait()


def leave_kernel(first, second):
    return pl.pallas_call(
        leave,
        out_shape=[jax.ShapeDtypeStruct(a.shape, a.dtype) for a in (first, second)],
        in_specs=[pl.BlockSpec(memory_space=pl.ANY)] * 2,
        out_specs=[pl.BlockSpec(memory_space=pl.ANY)] * 2,
        scratch_shapes=[pltpu.SemaphoreType.DMA((2,))],
        compiler_params=pltpu.CompilerParams(vmem_limit_bytes=2**20),
    )(first, second)


def iterate_kernel(slopes_in, moments_in, weights_in, parts, cols):
    mats, rows, wide = slopes_in.shape
    stages, side = mats // parts, rows * parts
    dma = pltpu.SemaphoreType.DMA
    n_rounds = max(1, max(neighbours(parts)[1].values()) - 1)
    return pl.pallas_call(
        functools.partial(kernel, stages, parts, cols),
        out_shape=[jax.ShapeDtypeStruct(slopes_in.shape, slopes_in.dtype)] * 2,
        in_specs=[pl.BlockSpec(memory_space=pltpu.HBM)] * 3,
        out_specs=[pl.BlockSpec(memory_space=pltpu.VMEM)] * 2,
        scratch_shapes=[
            pltpu.VMEM((2, stages, rows, wide), jnp.float32),
            pltpu.VMEM((2, mats, rows, wide), jnp.float32),
            *[pltpu.VMEM((mats, rows, wide), jnp.float32)] * 2,
            *[pltpu.VMEM((stages, parts, rows, wide), jnp.float32)] * 2,
            pltpu.VMEM((stages * cols, side, side), jnp.float32),
            dma((2,)), dma((1,)), dma((stages,)), dma((1,)), dma((1,)), dma((1 + parts // 2,)),
            dma((1,)), dma((2,)), pltpu.SemaphoreType.REGULAR((1,)), pltpu.SemaphoreType.REGULAR((n_rounds,)),
        ],
        compiler_params=pltpu.CompilerParams(collective_id=0, has_side_effects=True, vmem_limit_bytes=48 * 2**20),
    )(slopes_in, moments_in, weights_in)


def iterate_plain(new_momentum):
    moved = lax.all_to_all(new_momentum, "fsdp", split_axis=0, concat_axis=1, tiled=True)
    gram = lax.psum(jnp.einsum("mik,mjk->mij", moved, moved, precision=HIGH), "tp")
    dot = functools.partial(jnp.einsum, "mij,mjk->mik", precision=HIGH)
    total = polynomial(gram, dot, lambda a: jnp.sum(a, axis=(1, 2), keepdims=True))
    return lax.all_to_all(dot(total, moved), "fsdp", split_axis=1, concat_axis=0, tiled=True)


def body(parts, cols, slopes_in, moments_in, weights_in):
    if slopes_in.shape[1] % 8 == 0 and parts.bit_count() == 1 and parts // 2 > 2:
        new_momentum, new_weights = iterate_kernel(slopes_in, moments_in, weights_in, parts, cols)
        new_weights, new_momentum = leave_kernel(new_weights, new_momentum)
    else:
        new_momentum = hold_rate * moments_in + slopes_in
        new_weights = weights_in - learn_rate * iterate_plain(new_momentum)
    return (new_weights, new_momentum)


def solution(mesh):
    return jax.shard_map(
        functools.partial(body, mesh.shape["fsdp"], mesh.shape["tp"]),
        mesh=mesh,
        in_specs=(P(None, "fsdp", "tp"), P(None, "fsdp", "tp"), P(None, "fsdp", "tp")),
        out_specs=(P(None, "fsdp", "tp"), P(None, "fsdp", "tp")),
        check_vma=False,
    )
```

time: 97.4 us -> 96.7 us (level)
  no operation moved by 1% of the time
where the time goes in v2:
time: 96.7 us; the launch traced here: 96.6 us
  Pallas kernels  95.9 us (99%)
    pallas_call x1, Pallas kernels, iterate_kernel(): pl.pallas_call(functools.partial(kernel, stages, parts, cols), out_shape=...  93.9 us
    pallas_call x1, Pallas kernels, leave_kernel(): pl.pallas_call(leave, out_shape=[jax.ShapeDtypeStruct(a.shape, a.dtype) f...  2.03 us

profile of v2, /device:TPU:8, one launch (start us, length us, event | category | flops | bytes accessed | tf_op | source)
XLA Modules:
  0.0 96.6 jit_solution(1195977043045936187)
XLA Ops:
  0.6 93.9 %shard_map.50 = (f32[32,16,1024]{2,1,0:T(8,128)S(1)}, f32[32,16,1024]{2,1,0:T(8,128)S(1)}) custom-call(f32[32,16,1024]{2,1,0:T(8,128)} %slopes_ref.1, f32[32,16,1024]{2,1,0:T(8,128)} %moments_ref.1, f32[32,16,1024]{2,1,0:T(8,128)} %weights_ref.1), custom_call_target="tpu_custom_call" | custom-call | tf_op jit(solution)/shard_map/pallas_call | solution.py:285
  94.5 2.0 %shard_map.51 = (f32[32,16,1024]{2,1,0:T(8,128)}, f32[32,16,1024]{2,1,0:T(8,128)}) custom-call(f32[32,16,1024]{2,1,0:T(8,128)S(1)} %get-tuple-element.4.first_ref, f32[32,16,1024]{2,1,0:T(8,128)S(1)} %get-tuple-element.5.second_ref), custom_call_target="tpu_custom_call" | custom-call | tf_op jit(solution)/shard_map/pallas_call | solution.py:270

commit v3 on v2

--- a/solution.py
+++ b/solution.py
@@ -48,13 +48,10 @@
                 peer = peer + (1 - 2 * ((f // 2**bit) % 2)) * 2**bit
         return peer
 
-    near, level = neighbours(parts)
-    n_rounds = max(level.values()) - 1
-    if half > 2:
-        outer = jnp.where((f // 2 == half // 2 - 1) | (f // 2 == half // 2), 0, 1)
-    else:
-        outer = f * 0 + 1
-    first = near[0]
+    middle = (f // 2 == half // 2 - 1) | (f // 2 == half // 2)
+    outer = jnp.where(middle, 0, 1)
+    first, ahead = parts - 2, first_ref.shape[1]
+    known = [[], [half, half - 1, 2], [half + 1, 1], [parts - 1]]
     rest = [k for k in range(parts - 1, 0, -1) if k != first]
     inside = [pair(k) for k in range(half - 1, 0, -1)]
     outside = []
@@ -63,15 +60,13 @@
         x = f % 2 if j == half // 2 - 1 else 1
         outside += [2 * z + 1 - x, 2 * z + x]
 
-    def near_signal(sem):
-        for k in near:
+    def greet(sem, *ks):
+        for k in ks:
             pl.semaphore_signal(sem, inc=1, device_id={"fsdp": pair(k)}, device_id_type=MESH)
 
-    def tp_signal(sem):
-        @pl.when(outer == 1)
-        def _():
-            for k in range(1, cols):
-                pl.semaphore_signal(sem, inc=1, device_id={"tp": lax.rem(t + k, cols)}, device_id_type=MESH)
+    def greet_tp(sem):
+        for k in range(1, cols):
+            pl.semaphore_signal(sem, inc=1, device_id={"tp": lax.rem(t + k, cols)}, device_id_type=MESH)
 
     barrier = pltpu.get_barrier_semaphore()
 
@@ -81,11 +76,19 @@
         pltpu.make_async_copy(moments_ref.at[mat], first_ref.at[1, m], sem).start()
 
     load_first(0, loads.at[0])
-    near_signal(barrier)
-    for m in range(1, stages):
+    greet(barrier, first)
+
+    @pl.when(middle)
+    def _():
+        greet(barrier, 2)
+
+    for m in range(1, ahead):
         load_first(m, loads.at[1])
 
-    tp_signal(barrier)
+    @pl.when(outer == 1)
+    def _():
+        greet(barrier, 1)
+        greet_tp(barrier)
 
     def forward(m, peer):
         return pltpu.make_async_remote_copy(
@@ -119,51 +122,70 @@
             if k == 0:
                 x_ref[m, f] = value
 
+        @pl.when(m >= ahead)
+        def _():
+            mat = m * parts + pair(first)
+            momentum_ref[mat] = hold_rate * sm_ref[1, mat] + sm_ref[0, mat]
+
     settle(first_ref.at[:, 0], loads.at[0])
     momentum_ref[pair(first)] = hold_rate * first_ref[1, 0] + first_ref[0, 0]
     for which, src in enumerate((slopes_ref, moments_ref)):
         pltpu.make_async_copy(src, sm_ref.at[which], loads.at[0]).start()
-    pl.semaphore_wait(barrier, len(near) + outer * (cols - 1))
+    pl.semaphore_wait(barrier, 1 + outer * (cols + 1))
     forward(0, pair(first)).start()
-    settle(first_ref.at[:, pl.ds(1, stages - 1)], loads.at[1])
-    for m in range(1, stages):
+    if ahead > 1:
+        settle(first_ref.at[:, pl.ds(1, ahead - 1)], loads.at[1])
+    for m in range(1, ahead):
         momentum_ref[m * parts + pair(first)] = hold_rate * first_ref[1, m] + first_ref[0, m]
         forward(m, pair(first)).start()
-    tp_signal(met.at[0])
-    if n_rounds:
-        near_signal(rounds.at[0])
+
+    @pl.when(outer == 1)
+    def _():
+        greet(rounds.at[0], 2, 1, first)
+        greet_tp(met.at[0])
+
     settle(sm_ref, loads.at[0])
-    add(0)
-    for k in rest:
-        if level[k] == 1:
-            forward(0, pair(k)).start()
-
-    @pl.loop(1, stages)
+
+    @pl.loop(0, stages)
     def _(m):
         add(m)
 
     weights = pltpu.make_async_copy(weights_ref, w_ref, loads.at[1])
     weights.start()
-    for r in range(n_rounds):
-        pl.semaphore_wait(rounds.at[r], len(near))
-        if r == n_rounds - 1:
-            break
-        if r == n_rounds - 2:
-            @pl.when(outer == 1)
-            def _():
-                pl.semaphore_wait(met.at[0], cols - 1)
-        near_signal(rounds.at[r + 1])
-        for k in rest:
-            if level[k] == r + 2:
-                forward(0, pair(k)).start()
-    for k in rest:
-        if level[k] == n_rounds + 1 and n_rounds:
-            forward(0, pair(k)).start()
+
+    pl.semaphore_wait(rounds.at[0], 1 + outer)
+
+    @pl.when(outer == 1)
+    def _():
+        pl.semaphore_wait(met.at[0], cols - 1)
+        greet(rounds.at[1], 2, 1, first)
+
+    for k in known[1]:
+        forward(0, pair(k)).start()
+    pl.semaphore_wait(rounds.at[1], 1 + outer)
+
+    @pl.when(outer == 1)
+    def _():
+        greet(rounds.at[2], 2)
+
+    for k in known[2]:
+        forward(0, pair(k)).start()
+
+    @pl.when(middle)
+    def _():
+        pl.semaphore_wait(rounds.at[2], 1)
+
+    for k in known[3]:
+        forward(0, pair(k)).start()
 
     @pl.loop(1, stages)
     def _(m):
         for k in rest:
             forward(m, pair(k)).start()
+
+        @pl.when(m >= ahead)
+        def _():
+            forward(m, pair(first)).start()
 
     dot = functools.partial(jnp.dot, precision=HIGH, preferred_element_type=jnp.float32)
 
@@ -243,21 +265,6 @@
     settle(g_ref.at[pl.ds(0, stages * (cols - 1))], gsend.at[0])
 
 
-def neighbours(parts):
-    near = [k for k in (parts - 2, *(2**b for b in range(1, parts.bit_length() - 2)), 1) if k]
-    near = list(dict.fromkeys(near))
-    level, edge = {0: 0}, [0]
-    while edge:
-        found = {}
-        for k in edge:
-            for step in near:
-                if k ^ step not in level:
-                    found[k ^ step] = level[k] + 1
-        level.update(found)
-        edge = list(found)
-    return near, level
-
-
 def leave(first_ref, second_ref, first_out, second_out, sems):
     copies = [pltpu.make_async_copy(first_ref, first_out, sems.at[0]), pltpu.make_async_copy(second_ref, second_out, sems.at[1])]
     for copy in copies:
@@ -281,20 +288,20 @@
     mats, rows, wide = slopes_in.shape
     stages, side = mats // parts, rows * parts
     dma = pltpu.SemaphoreType.DMA
-    n_rounds = max(1, max(neighbours(parts)[1].values()) - 1)
+    ahead = (stages + 1) // 2
     return pl.pallas_call(
         functools.partial(kernel, stages, parts, cols),
         out_shape=[jax.ShapeDtypeStruct(slopes_in.shape, slopes_in.dtype)] * 2,
         in_specs=[pl.BlockSpec(memory_space=pltpu.HBM)] * 3,
         out_specs=[pl.BlockSpec(memory_space=pltpu.VMEM)] * 2,
         scratch_shapes=[
-            pltpu.VMEM((2, stages, rows, wide), jnp.float32),
+            pltpu.VMEM((2, ahead, rows, wide), jnp.float32),
             pltpu.VMEM((2, mats, rows, wide), jnp.float32),
             *[pltpu.VMEM((mats, rows, wide), jnp.float32)] * 2,
             *[pltpu.VMEM((stages, parts, rows, wide), jnp.float32)] * 2,
             pltpu.VMEM((stages * cols, side, side), jnp.float32),
             dma((2,)), dma((1,)), dma((stages,)), dma((1,)), dma((1,)), dma((1 + parts // 2,)),
-            dma((1,)), dma((2,)), pltpu.SemaphoreType.REGULAR((1,)), pltpu.SemaphoreType.REGULAR((n_rounds,)),
+            dma((1,)), dma((2,)), pltpu.SemaphoreType.REGULAR((1,)), pltpu.SemaphoreType.REGULAR((3,)),
         ],
         compiler_params=pltpu.CompilerParams(collective_id=0, has_side_effects=True, vmem_limit_bytes=48 * 2**20),
     )(slopes_in, moments_in, weights_in)
@@ -309,7 +316,7 @@
 
 
 def body(parts, cols, slopes_in, moments_in, weights_in):
-    if slopes_in.shape[1] % 8 == 0 and parts.bit_count() == 1 and parts // 2 > 2:
+    if slopes_in.shape[1] % 8 == 0 and parts // 4 == 2 and parts % 4 == 0:
         new_momentum, new_weights = iterate_kernel(slopes_in, moments_in, weights_in, parts, cols)
         new_weights, new_momentum = leave_kernel(new_weights, new_momentum)
     else:

time: 96.7 us -> 96.2 us (level)
  no operation moved by 1% of the time
where the time goes in v3:
time: 96.2 us; the launch traced here: 96 us
  Pallas kernels  95.3 us (99%)
    pallas_call x1, Pallas kernels, iterate_kernel(): pl.pallas_call(functools.partial(kernel, stages, parts, cols), out_shape=...  93.3 us
    pallas_call x1, Pallas kernels, leave_kernel(): pl.pallas_call(leave, out_shape=[jax.ShapeDtypeStruct(a.shape, a.dtype) f...  2.03 us

profile of v3, /device:TPU:8, one launch (start us, length us, event | category | flops | bytes accessed | tf_op | source)
XLA Modules:
  0.0 96.0 jit_solution(18277722988457355042)
XLA Ops:
  0.6 93.3 %shard_map.50 = (f32[32,16,1024]{2,1,0:T(8,128)S(1)}, f32[32,16,1024]{2,1,0:T(8,128)S(1)}) custom-call(f32[32,16,1024]{2,1,0:T(8,128)} %slopes_ref.1, f32[32,16,1024]{2,1,0:T(8,128)} %moments_ref.1, f32[32,16,1024]{2,1,0:T(8,128)} %weights_ref.1), custom_call_target="tpu_custom_call" | custom-call | tf_op jit(solution)/shard_map/pallas_call | solution.py:292
  94.0 2.0 %shard_map.51 = (f32[32,16,1024]{2,1,0:T(8,128)}, f32[32,16,1024]{2,1,0:T(8,128)}) custom-call(f32[32,16,1024]{2,1,0:T(8,128)S(1)} %get-tuple-element.4.first_ref, f32[32,16,1024]{2,1,0:T(8,128)S(1)} %get-tuple-element.5.second_ref), custom_call_target="tpu_custom_call" | custom-call | tf_op jit(solution)/shard_map/pallas_call | solution.py:277

commit v4 on v3

--- a/solution.py
+++ b/solution.py
@@ -40,6 +40,7 @@
     side, mats, half, last = parts * rows, stages * parts, parts // 2, stages - 1
     f, t = lax.axis_index("fsdp"), lax.axis_index("tp")
     upper = f // half
+    soon, late = (slice(None), pl.ds(0, wide // 4)), (slice(None), pl.ds(wide // 4, wide - wide // 4))
 
     def pair(k):
         peer = f
@@ -72,8 +73,10 @@
 
     def load_first(m, sem):
         mat = m * parts + pair(first)
-        pltpu.make_async_copy(slopes_ref.at[mat], first_ref.at[0, m], sem).start()
-        pltpu.make_async_copy(moments_ref.at[mat], first_ref.at[1, m], sem).start()
+        for piece in range(2):
+            part = pl.ds(piece * rows // 2, rows // 2)
+            pltpu.make_async_copy(slopes_ref.at[mat, part], first_ref.at[0, m, part], sem).start()
+            pltpu.make_async_copy(moments_ref.at[mat, part], first_ref.at[1, m, part], sem).start()
 
     load_first(0, loads.at[0])
     greet(barrier, first)
@@ -97,9 +100,9 @@
             device_id={"fsdp": peer}, device_id_type=MESH,
         )
 
-    def backward(m, peer, recv):
+    def backward(m, peer, recv, *part):
         return pltpu.make_async_remote_copy(
-            src_ref=y_ref.at[m, peer], dst_ref=back_ref.at[m * parts + f],
+            src_ref=y_ref.at[m, peer, *part], dst_ref=back_ref.at[m * parts + f, *part],
             send_sem=bsend.at[0], recv_sem=recv,
             device_id={"fsdp": peer}, device_id_type=MESH,
         )
@@ -222,9 +225,11 @@
             for peer in outside[1:-1]:
                 backward(m, peer, blast.at[1 + f % half]).start()
 
+            backward(m, outside[-1], blast.at[1 + f % half], *soon).start()
+
             @pl.when(t % 2 == 0)
             def _():
-                backward(m, outside[-1], blast.at[1 + f % half]).start()
+                backward(m, outside[-1], blast.at[1 + f % half], *late).start()
 
     def finish(m, peers):
         for peer in peers:
@@ -244,7 +249,7 @@
     @pl.when(t % 2 == 1)
     def _():
         settle(back_ref.at[pl.ds(0, mats - stages - 1)], bsend.at[0])
-        backward(last, outside[-1], blast.at[1 + f % half]).start()
+        backward(last, outside[-1], blast.at[1 + f % half], *late).start()
 
     if inside:
         settle(back_ref.at[pl.ds(0, len(inside))], blast.at[0])

time: 96.2 us -> 96.3 us (level)
  no operation moved by 1% of the time
where the time goes in v4:
time: 96.3 us; the launch traced here: 96 us
  Pallas kernels  95.3 us (99%)
    pallas_call x1, Pallas kernels, iterate_kernel(): pl.pallas_call(functools.partial(kernel, stages, parts, cols), out_shape=...  93.3 us
    pallas_call x1, Pallas kernels, leave_kernel(): pl.pallas_call(leave, out_shape=[jax.ShapeDtypeStruct(a.shape, a.dtype) f...  2.03 us

profile of v4, /device:TPU:8, one launch (start us, length us, event | category | flops | bytes accessed | tf_op | source)
XLA Modules:
  0.0 96.0 jit_solution(14243257039617123502)
XLA Ops:
  0.6 93.3 %shard_map.50 = (f32[32,16,1024]{2,1,0:T(8,128)S(1)}, f32[32,16,1024]{2,1,0:T(8,128)S(1)}) custom-call(f32[32,16,1024]{2,1,0:T(8,128)} %slopes_ref.1, f32[32,16,1024]{2,1,0:T(8,128)} %moments_ref.1, f32[32,16,1024]{2,1,0:T(8,128)} %weights_ref.1), custom_call_target="tpu_custom_call" | custom-call | tf_op jit(solution)/shard_map/pallas_call | solution.py:297
  93.9 2.0 %shard_map.51 = (f32[32,16,1024]{2,1,0:T(8,128)}, f32[32,16,1024]{2,1,0:T(8,128)}) custom-call(f32[32,16,1024]{2,1,0:T(8,128)S(1)} %get-tuple-element.4.first_ref, f32[32,16,1024]{2,1,0:T(8,128)S(1)} %get-tuple-element.5.second_ref), custom_call_target="tpu_custom_call" | custom-call | tf_op jit(solution)/shard_map/pallas_call | solution.py:282

commit v5 on v4

--- a/solution.py
+++ b/solution.py
@@ -220,10 +220,10 @@
             for peer in inside:
                 backward(m, peer, blast.at[0]).start()
             backward(m, outside[0], blast.at[1 + f % half]).start()
+            for peer in outside[1:-1]:
+                backward(m, peer, blast.at[1 + f % half]).start()
             if last:
                 backward(last - 1, outside[-1], brecv.at[0]).start()
-            for peer in outside[1:-1]:
-                backward(m, peer, blast.at[1 + f % half]).start()
 
             backward(m, outside[-1], blast.at[1 + f % half], *soon).start()
 
@@ -239,17 +239,17 @@
     weights.wait()
     for m in range(stages):
         new_ref[m * parts + f] = w_ref[m * parts + f] - learn_rate * y_ref[m, f]
+    @pl.when(t % 2 == 1)
+    def _():
+        settle(back_ref.at[pl.ds(0, mats - stages - 1)], bsend.at[0])
+        backward(last, outside[-1], blast.at[1 + f % half], *late).start()
+
     if last:
         settle(back_ref.at[pl.ds(0, last * (parts - 1))], brecv.at[0])
 
         @pl.loop(0, last)
         def _(m):
             finish(m, inside + outside)
-
-    @pl.when(t % 2 == 1)
-    def _():
-        settle(back_ref.at[pl.ds(0, mats - stages - 1)], bsend.at[0])
-        backward(last, outside[-1], blast.at[1 + f % half], *late).start()
 
     if inside:
         settle(back_ref.at[pl.ds(0, len(inside))], blast.at[0])

time: 96.3 us -> 96.1 us (level)
  no operation moved by 1% of the time
where the time goes in v5:
time: 96.1 us; the launch traced here: 96 us
  Pallas kernels  95.3 us (99%)
    pallas_call x1, Pallas kernels, iterate_kernel(): pl.pallas_call(functools.partial(kernel, stages, parts, cols), out_shape=...  93.3 us
    pallas_call x1, Pallas kernels, leave_kernel(): pl.pallas_call(leave, out_shape=[jax.ShapeDtypeStruct(a.shape, a.dtype) f...  2.03 us

profile of v5, /device:TPU:8, one launch (start us, length us, event | category | flops | bytes accessed | tf_op | source)
XLA Modules:
  0.0 96.0 jit_solution(173670088957385151)
XLA Ops:
  0.6 93.3 %shard_map.50 = (f32[32,16,1024]{2,1,0:T(8,128)S(1)}, f32[32,16,1024]{2,1,0:T(8,128)S(1)}) custom-call(f32[32,16,1024]{2,1,0:T(8,128)} %slopes_ref.1, f32[32,16,1024]{2,1,0:T(8,128)} %moments_ref.1, f32[32,16,1024]{2,1,0:T(8,128)} %weights_ref.1), custom_call_target="tpu_custom_call" | custom-call | tf_op jit(solution)/shard_map/pallas_call | solution.py:297
  93.9 2.0 %shard_map.51 = (f32[32,16,1024]{2,1,0:T(8,128)}, f32[32,16,1024]{2,1,0:T(8,128)}) custom-call(f32[32,16,1024]{2,1,0:T(8,128)S(1)} %get-tuple-element.4.first_ref, f32[32,16,1024]{2,1,0:T(8,128)S(1)} %get-tuple-element.5.second_ref), custom_call_target="tpu_custom_call" | custom-call | tf_op jit(solution)/shard_map/pallas_call | solution.py:282

commit v6 on v5

--- a/solution.py
+++ b/solution.py
@@ -34,7 +34,7 @@
 
 def kernel(
     stages, parts, cols, slopes_ref, moments_ref, weights_ref, momentum_ref, new_ref,
-    first_ref, sm_ref, w_ref, back_ref, x_ref, y_ref, g_ref, loads, fsend, frecv, bsend, brecv, blast, gsend, grecv, met, rounds,
+    first_ref, sm_ref, w_ref, back_ref, x_ref, y_ref, g_ref, loads, fsend, frecv, bsend, brecv, blast, gsend, grecv, rounds,
 ):
     rows, wide = momentum_ref.shape[1:]
     side, mats, half, last = parts * rows, stages * parts, parts // 2, stages - 1
@@ -145,7 +145,7 @@
     @pl.when(outer == 1)
     def _():
         greet(rounds.at[0], 2, 1, first)
-        greet_tp(met.at[0])
+        greet_tp(rounds.at[0])
 
     settle(sm_ref, loads.at[0])
 
@@ -156,11 +156,10 @@
     weights = pltpu.make_async_copy(weights_ref, w_ref, loads.at[1])
     weights.start()
 
-    pl.semaphore_wait(rounds.at[0], 1 + outer)
+    pl.semaphore_wait(rounds.at[0], 1 + outer * cols)
 
     @pl.when(outer == 1)
     def _():
-        pl.semaphore_wait(met.at[0], cols - 1)
         greet(rounds.at[1], 2, 1, first)
 
     for k in known[1]:
@@ -218,18 +217,18 @@
         @pl.when(m == last)
         def _():
             for peer in inside:
-                backward(m, peer, blast.at[0]).start()
-            backward(m, outside[0], blast.at[1 + f % half]).start()
+                backward(m, peer, brecv.at[0]).start()
+            backward(m, outside[0], blast.at[f % half]).start()
             for peer in outside[1:-1]:
-                backward(m, peer, blast.at[1 + f % half]).start()
+                backward(m, peer, blast.at[f % half]).start()
             if last:
                 backward(last - 1, outside[-1], brecv.at[0]).start()
 
-            backward(m, outside[-1], blast.at[1 + f % half], *soon).start()
+            backward(m, outside[-1], blast.at[f % half], *soon).start()
 
             @pl.when(t % 2 == 0)
             def _():
-                backward(m, outside[-1], blast.at[1 + f % half], *late).start()
+                backward(m, outside[-1], blast.at[f % half], *late).start()
 
     def finish(m, peers):
         for peer in peers:
@@ -242,20 +241,17 @@
     @pl.when(t % 2 == 1)
     def _():
         settle(back_ref.at[pl.ds(0, mats - stages - 1)], bsend.at[0])
-        backward(last, outside[-1], blast.at[1 + f % half], *late).start()
-
-    if last:
-        settle(back_ref.at[pl.ds(0, last * (parts - 1))], brecv.at[0])
-
-        @pl.loop(0, last)
-        def _(m):
-            finish(m, inside + outside)
-
-    if inside:
-        settle(back_ref.at[pl.ds(0, len(inside))], blast.at[0])
-        finish(last, inside)
+        backward(last, outside[-1], blast.at[f % half], *late).start()
+
+    settle(back_ref.at[pl.ds(0, last * (parts - 1) + len(inside))], brecv.at[0])
+    finish(last, inside)
+
+    @pl.loop(0, last)
+    def _(m):
+        finish(m, inside + outside)
+
     for peer in outside:
-        settle(back_ref.at[last * parts + peer], blast.at[1 + peer % half])
+        settle(back_ref.at[last * parts + peer], blast.at[peer % half])
         finish(last, [peer])
 
     settle(momentum_ref.at[pl.ds(0, mats - stages)], fsend.at[0])
@@ -305,8 +301,8 @@
             *[pltpu.VMEM((mats, rows, wide), jnp.float32)] * 2,
             *[pltpu.VMEM((stages, parts, rows, wide), jnp.float32)] * 2,
             pltpu.VMEM((stages * cols, side, side), jnp.float32),
-            dma((2,)), dma((1,)), dma((stages,)), dma((1,)), dma((1,)), dma((1 + parts // 2,)),
-            dma((1,)), dma((2,)), pltpu.SemaphoreType.REGULAR((1,)), pltpu.SemaphoreType.REGULAR((3,)),
+            dma((2,)), dma((1,)), dma((stages,)), dma((1,)), dma((1,)), dma((parts // 2,)),
+            dma((1,)), dma((2,)), pltpu.SemaphoreType.REGULAR((3,)),
         ],
         compiler_params=pltpu.CompilerParams(collective_id=0, has_side_effects=True, vmem_limit_bytes=48 * 2**20),
     )(slopes_in, moments_in, weights_in)

time: 96.1 us -> 96.1 us (level)
  no operation moved by 1% of the time
where the time goes in v6:
time: 96.1 us; the launch traced here: 95.9 us
  Pallas kernels  95.3 us (99%)
    pallas_call x1, Pallas kernels, iterate_kernel(): pl.pallas_call(functools.partial(kernel, stages, parts, cols), out_shape=...  93.3 us
    pallas_call x1, Pallas kernels, leave_kernel(): pl.pallas_call(leave, out_shape=[jax.ShapeDtypeStruct(a.shape, a.dtype) f...  2.03 us

profile of v6, /device:TPU:8, one launch (start us, length us, event | category | flops | bytes accessed | tf_op | source)
XLA Modules:
  0.0 95.9 jit_solution(4229452799496358055)
XLA Ops:
  0.6 93.3 %shard_map.50 = (f32[32,16,1024]{2,1,0:T(8,128)S(1)}, f32[32,16,1024]{2,1,0:T(8,128)S(1)}) custom-call(f32[32,16,1024]{2,1,0:T(8,128)} %slopes_ref.1, f32[32,16,1024]{2,1,0:T(8,128)} %moments_ref.1, f32[32,16,1024]{2,1,0:T(8,128)} %weights_ref.1), custom_call_target="tpu_custom_call" | custom-call | tf_op jit(solution)/shard_map/pallas_call | solution.py:293
  93.9 2.0 %shard_map.51 = (f32[32,16,1024]{2,1,0:T(8,128)}, f32[32,16,1024]{2,1,0:T(8,128)}) custom-call(f32[32,16,1024]{2,1,0:T(8,128)S(1)} %get-tuple-element.4.first_ref, f32[32,16,1024]{2,1,0:T(8,128)S(1)} %get-tuple-element.5.second_ref), custom_call_target="tpu_custom_call" | custom-call | tf_op jit(solution)/shard_map/pallas_call | solution.py:278

commit v7 on v6

--- a/solution.py
+++ b/solution.py
@@ -243,6 +243,8 @@
         settle(back_ref.at[pl.ds(0, mats - stages - 1)], bsend.at[0])
         backward(last, outside[-1], blast.at[f % half], *late).start()
 
+    settle(momentum_ref.at[pl.ds(0, mats - stages)], fsend.at[0])
+    settle(g_ref.at[pl.ds(0, stages * (cols - 1))], gsend.at[0])
     settle(back_ref.at[pl.ds(0, last * (parts - 1) + len(inside))], brecv.at[0])
     finish(last, inside)
 
@@ -254,7 +256,6 @@
         settle(back_ref.at[last * parts + peer], blast.at[peer % half])
         finish(last, [peer])
 
-    settle(momentum_ref.at[pl.ds(0, mats - stages)], fsend.at[0])
     @pl.when(t % 2 == 1)
     def _():
         settle(back_ref.at[pl.ds(0, 1)], bsend.at[0])
@@ -262,8 +263,6 @@
     @pl.when(t % 2 == 0)
     def _():
         settle(back_ref.at[pl.ds(0, mats - stages)], bsend.at[0])
-
-    settle(g_ref.at[pl.ds(0, stages * (cols - 1))], gsend.at[0])
 
 
 def leave(first_ref, second_ref, first_out, second_out, sems):

time: 96.1 us -> 96.1 us (level)
  no operation moved by 1% of the time
where the time goes in v7:
time: 96.1 us; the launch traced here: 95.9 us
  Pallas kernels  95.3 us (99%)
    pallas_call x1, Pallas kernels, iterate_kernel(): pl.pallas_call(functools.partial(kernel, stages, parts, cols), out_shape=...  93.3 us
    pallas_call x1, Pallas kernels, leave_kernel(): pl.pallas_call(leave, out_shape=[jax.ShapeDtypeStruct(a.shape, a.dtype) f...  2.03 us

profile of v7, /device:TPU:8, one launch (start us, length us, event | category | flops | bytes accessed | tf_op | source)
XLA Modules:
  0.0 95.9 jit_solution(13198813172685955179)
XLA Ops:
  0.6 93.3 %shard_map.50 = (f32[32,16,1024]{2,1,0:T(8,128)S(1)}, f32[32,16,1024]{2,1,0:T(8,128)S(1)}) custom-call(f32[32,16,1024]{2,1,0:T(8,128)} %slopes_ref.1, f32[32,16,1024]{2,1,0:T(8,128)} %moments_ref.1, f32[32,16,1024]{2,1,0:T(8,128)} %weights_ref.1), custom_call_target="tpu_custom_call" | custom-call | tf_op jit(solution)/shard_map/pallas_call | solution.py:292
  93.9 2.0 %shard_map.51 = (f32[32,16,1024]{2,1,0:T(8,128)}, f32[32,16,1024]{2,1,0:T(8,128)}) custom-call(f32[32,16,1024]{2,1,0:T(8,128)S(1)} %get-tuple-element.4.first_ref, f32[32,16,1024]{2,1,0:T(8,128)S(1)} %get-tuple-element.5.second_ref), custom_call_target="tpu_custom_call" | custom-call | tf_op jit(solution)/shard_map/pallas_call | solution.py:277

commit v8 on v7

--- a/solution.py
+++ b/solution.py
@@ -51,6 +51,7 @@
 
     middle = (f // 2 == half // 2 - 1) | (f // 2 == half // 2)
     outer = jnp.where(middle, 0, 1)
+    mine = (1 - outer) * (1 + f % 2)
     first, ahead = parts - 2, first_ref.shape[1]
     known = [[], [half, half - 1, 2], [half + 1, 1], [parts - 1]]
     rest = [k for k in range(parts - 1, 0, -1) if k != first]
@@ -218,17 +219,17 @@
         def _():
             for peer in inside:
                 backward(m, peer, brecv.at[0]).start()
-            backward(m, outside[0], blast.at[f % half]).start()
+            backward(m, outside[0], blast.at[mine]).start()
             for peer in outside[1:-1]:
-                backward(m, peer, blast.at[f % half]).start()
+                backward(m, peer, blast.at[mine]).start()
             if last:
                 backward(last - 1, outside[-1], brecv.at[0]).start()
 
-            backward(m, outside[-1], blast.at[f % half], *soon).start()
+            backward(m, outside[-1], blast.at[mine], *soon).start()
 
             @pl.when(t % 2 == 0)
             def _():
-                backward(m, outside[-1], blast.at[f % half], *late).start()
+                backward(m, outside[-1], blast.at[mine], *late).start()
 
     def finish(m, peers):
         for peer in peers:
@@ -241,7 +242,7 @@
     @pl.when(t % 2 == 1)
     def _():
         settle(back_ref.at[pl.ds(0, mats - stages - 1)], bsend.at[0])
-        backward(last, outside[-1], blast.at[f % half], *late).start()
+        backward(last, outside[-1], blast.at[mine], *late).start()
 
     settle(momentum_ref.at[pl.ds(0, mats - stages)], fsend.at[0])
     settle(g_ref.at[pl.ds(0, stages * (cols - 1))], gsend.at[0])
@@ -252,8 +253,10 @@
     def _(m):
         finish(m, inside + outside)
 
-    for peer in outside:
-        settle(back_ref.at[last * parts + peer], blast.at[peer % half])
+    settle(back_ref.at[pl.ds(0, 2)], blast.at[0])
+    finish(last, outside[:2])
+    for peer in outside[2:]:
+        settle(back_ref.at[last * parts + peer], blast.at[1 + peer % 2])
         finish(last, [peer])
 
     @pl.when(t % 2 == 1)
@@ -300,7 +303,7 @@
             *[pltpu.VMEM((mats, rows, wide), jnp.float32)] * 2,
             *[pltpu.VMEM((stages, parts, rows, wide), jnp.float32)] * 2,
             pltpu.VMEM((stages * cols, side, side), jnp.float32),
-            dma((2,)), dma((1,)), dma((stages,)), dma((1,)), dma((1,)), dma((parts // 2,)),
+            dma((2,)), dma((1,)), dma((stages,)), dma((1,)), dma((1,)), dma((3,)),
             dma((1,)), dma((2,)), pltpu.SemaphoreType.REGULAR((3,)),
         ],
         compiler_params=pltpu.CompilerParams(collective_id=0, has_side_effects=True, vmem_limit_bytes=48 * 2**20),

time: 96.1 us -> 96.1 us (level)
  no operation moved by 1% of the time
where the time goes in v8:
time: 96.1 us; the launch traced here: 95.9 us
  Pallas kernels  95.3 us (99%)
    pallas_call x1, Pallas kernels, iterate_kernel(): pl.pallas_call(functools.partial(kernel, stages, parts, cols), out_shape=...  93.3 us
    pallas_call x1, Pallas kernels, leave_kernel(): pl.pallas_call(leave, out_shape=[jax.ShapeDtypeStruct(a.shape, a.dtype) f...  2.03 us

profile of v8, /device:TPU:8, one launch (start us, length us, event | category | flops | bytes accessed | tf_op | source)
XLA Modules:
  0.0 95.9 jit_solution(13655839089415167280)
XLA Ops:
  0.6 93.3 %shard_map.50 = (f32[32,16,1024]{2,1,0:T(8,128)S(1)}, f32[32,16,1024]{2,1,0:T(8,128)S(1)}) custom-call(f32[32,16,1024]{2,1,0:T(8,128)} %slopes_ref.1, f32[32,16,1024]{2,1,0:T(8,128)} %moments_ref.1, f32[32,16,1024]{2,1,0:T(8,128)} %weights_ref.1), custom_call_target="tpu_custom_call" | custom-call | tf_op jit(solution)/shard_map/pallas_call | solution.py:295
  93.9 2.0 %shard_map.51 = (f32[32,16,1024]{2,1,0:T(8,128)}, f32[32,16,1024]{2,1,0:T(8,128)}) custom-call(f32[32,16,1024]{2,1,0:T(8,128)S(1)} %get-tuple-element.4.first_ref, f32[32,16,1024]{2,1,0:T(8,128)S(1)} %get-tuple-element.5.second_ref), custom_call_target="tpu_custom_call" | custom-call | tf_op jit(solution)/shard_map/pallas_call | solution.py:280
